TPU v7x, 32 devices: a whole 2x2x4 slice. The times are simulated.
32 devices in a mesh: px: 8 (over z, y), py: 4 (over x, core).
Axes of the slice: x: 2, y: 2, z: 4, core: 2. Of those that a mesh axis runs over, the one named last changes fastest.
Arguments:
- mode_field: float32 [64, 512, 1024], P(None, 'px', 'py'), may hold values from -1 to 1
- forcing: float32 [64, 512, 1024], P(None, 'px', 'py'), may hold values from -8 to 8
- visc_base: float32 [64, 1024, 512], P('py', 'px'), may hold values from 0.1 to 3
- depth_inverse: float32 [1024, 64, 64], P('py'), may hold values from -1 to 2, as said below
Outputs:
- mode_field_out: float32 [64, 512, 1024], P(None, 'px', 'py')
- residual_norms: float32 [2], replicated
Inputs may be any that keep to these rules, and one draw needn't show every extreme that they name: `depth_inverse`: each matrix has its diagonal between 0.5 and 1.5 and off-diagonal entries of magnitude at most 0.4 / sqrt(64).
All inputs are finite; a program needn't handle non-finite values.
Results may differ from a plain program's by a relative error of at most 0.0001.
Values sent between devices are 32-bit elements; how exact they have to be, the bound alone decides.
A program may use at most 128 MiB of HBM per device.

v0:
```python
import math
import jax
import jax.numpy as jnp
from jax import lax
from jax.sharding import PartitionSpec as P

ITERS = 2


def depth_tables(count):
    index = jnp.arange(count, dtype=jnp.float32)
    angle = jnp.pi * index[:, None] * index[None, :] / (count - 1)
    ends = jnp.where((index == 0) | (index == count - 1), 2.0, 1.0)
    forward = jnp.cos(angle)
    backward = 2.0 / (count - 1) * jnp.cos(angle) / (ends[:, None] * ends[None, :])
    return (forward, backward)


def hartley_table(count):
    index = jnp.arange(count, dtype=jnp.int32)
    phase = index[:, None] * index[None, :] % count
    angle = phase.astype(jnp.float32) * (2.0 * math.pi / count)
    return (jnp.cos(angle) + jnp.sin(angle)) / math.sqrt(count)


def wave_square(index, count):
    folded = jnp.minimum(index, count - index).astype(jnp.float32)
    scaled = 2.0 * jnp.pi * folded / count
    return scaled * scaled


def local(mode_field, forcing, visc_base, depth_inverse):
    depth_count = mode_field.shape[0]
    rows_y = mode_field.shape[1]
    cols_x = mode_field.shape[2]
    total_y = rows_y * lax.axis_size("px")
    total_x = cols_x * lax.axis_size("py")
    cell_total = depth_count * total_y * total_x
    forward, backward = depth_tables(depth_count)
    table_x = hartley_table(total_x)
    table_y = hartley_table(total_y)
    index_y = lax.axis_index("px") * rows_y + jnp.arange(rows_y, dtype=jnp.int32)
    index_x = lax.axis_index("py") * cols_x + jnp.arange(cols_x, dtype=jnp.int32)
    lateral = wave_square(index_y, total_y)[:, None] + wave_square(index_x, total_x)[None, :]
    highest = lax.Precision.HIGHEST
    field = mode_field
    partials = []
    for sweep in range(ITERS):
        points = jnp.einsum("jm,myx->jyx", forward, field, precision=highest)
        lines = lax.all_to_all(points, "py", split_axis=0, concat_axis=2, tiled=True)
        lines = jnp.einsum("zyk,xk->zyx", lines, table_x, precision=highest)
        columns = lax.all_to_all(lines, "px", split_axis=2, concat_axis=1, tiled=True)
        physical = jnp.einsum("zkx,yk->zxy", columns, table_y, precision=highest)
        stress = visc_base * jnp.power(1.0 + physical * physical, -1.0 / 3.0) * physical
        returned = jnp.einsum("zxy,ky->zkx", stress, table_y, precision=highest)
        returned = lax.all_to_all(returned, "px", split_axis=1, concat_axis=2, tiled=True)
        returned = jnp.einsum("zyx,kx->zyk", returned, table_x, precision=highest)
        spectral = lax.all_to_all(returned, "py", split_axis=2, concat_axis=0, tiled=True)
        viscous = jnp.einsum("mj,jyx->myx", backward, spectral, precision=highest)
        residual = forcing - (lateral * field + viscous)
        squares = jnp.sum(residual * residual)
        partials.append(squares)
        correction = jnp.einsum("xmn,nyx->myx", depth_inverse, residual, precision=highest)
        field = field + correction / (1.0 + lateral)
    norm_values = lax.psum(jnp.stack(partials), ("px", "py")) / cell_total
    return (field, norm_values)


def solution(mesh):
    placed = (P(None, "px", "py"), P(None, "px", "py"), P("py", "px", None), P("py", None, None))
    return jax.shard_map(
        local, mesh=mesh, in_specs=placed, out_specs=(P(None, "px", "py"), P()), check_vma=False
    )
```

profile of v0, /device:TPU:0, one launch (start us, length us, event | category | flops | bytes accessed | tf_op | source)
XLA Modules:
  0.0 1180.5 jit_solution(4981128345261432026)
XLA Ops:
  18.6 17.7 %fusion.151 = f32[1024,1024,1]{1,0,2:T(8,128)} fusion(), kind=kLoop, calls=%fused_computation.17.clone | loop fusion | flops 16777216 | bytes 4194304 | tf_op jit(solution)/shard_map/zyk,xk->zyx/dot_general | solution.py:51
  36.3 31.2 %all-to-all-done = f32[64,64,256]{2,1,0:T(8,128)} async-done(((f32[64,64,256]{2,1,0:T(8,128)}), f32[64,64,256]{2,1,0:T(8,128)}, u32[]{:S(2)}, u32[]{:S(2)}) %all-to-all-start) | async-done | bytes 4194336 | tf_op jit(solution)/shard_map/all_to_all | solution.py:50
  80.3 17.6 %fusion.11 = f32[16,64,1024]{2,1,0:T(8,128)} fusion(f32[16,64,1024]{2,1,0:T(8,128)} %all_to_all.107, f32[1024,1024,1]{1,0,2:T(8,128)} %fusion.151), kind=kOutput, calls=%fused_computation.16 | convolution fusion | flops 12884901888 | bytes 12582912 | tf_op jit(solution)/shard_map/zyk,xk->zyx/dot_general | solution.py:51
  115.9 99.8 %all_to_all.144 = f32[8,1,131072]{2,1,0:T(1,128)} all-to-all(f32[8,1,131072]{2,1,0:T(1,128)} %reshape.101), channel_id=1, replica_groups=mesh['px'=8,'py'=4] {'px'}, dimensions={0} | all-to-all | bytes 8388608 | tf_op jit(solution)/shard_map/all_to_all | solution.py:52
  245.9 19.7 %fusion.47 = f32[16,128,512]{2,1,0:T(8,128)S(1)} fusion(f32[16,512,128]{2,1,0:T(8,128)} %bitcast.126), kind=kOutput, calls=%fused_computation.60 | convolution fusion | flops 6446645248 | bytes 8388608 | tf_op jit(solution)/shard_map/zkx,yk->zxy/dot_general | solution.py:53
  265.6 16.7 %fusion.30 = f32[16,512,128]{2,1,0:T(8,128)S(1)} fusion(f32[16,128,512]{2,1,0:T(8,128)S(1)} %fusion.47, f32[16,128,512]{2,1,0:T(8,128)S(1)} %copy-done.1), kind=kOutput, calls=%fused_computation.44 | convolution fusion | flops 6450839552 | bytes 12582912 | tf_op jit(solution)/shard_map/zxy,ky->zkx/dot_general | solution.py:55
  291.5 17.7 %fusion.149 = f32[1024,1024,1]{1,0,2:T(8,128)} fusion(), kind=kLoop, calls=%fused_computation.15.clone | loop fusion | flops 16777216 | bytes 4194304 | tf_op jit(solution)/shard_map/zyx,kx->zyk/dot_general | solution.py:57
  309.2 74.6 %all-to-all-done.2 = f32[16,512,128]{2,0,1:T(8,128)} async-done(((f32[16,512,128]{2,0,1:T(8,128)}), f32[16,512,128]{2,0,1:T(8,128)}, u32[]{:S(2)}, u32[]{:S(2)}) %all-to-all-start.2) | async-done | bytes 4194336 | tf_op jit(solution)/shard_map/all_to_all | solution.py:56
  395.3 17.6 %fusion.9 = f32[16,64,1024]{2,1,0:T(8,128)} fusion(f32[16,64,1024]{2,1,0:T(8,128)} %all_to_all.115, f32[1024,1024,1]{1,0,2:T(8,128)} %fusion.149), kind=kOutput, calls=%fused_computation.14 | convolution fusion | flops 12884901888 | bytes 12582912 | tf_op jit(solution)/shard_map/zyx,kx->zyk/dot_general | solution.py:57
  443.9 38.9 %all-to-all-done.3 = f32[4,1,262144]{2,1,0:T(1,128)} async-done(((f32[4,1,262144]{2,1,0:T(1,128)}), f32[4,1,262144]{2,1,0:T(1,128)}, u32[]{:S(2)}, u32[]{:S(2)}) %all-to-all-start.3) | async-done | bytes 4194336 | tf_op jit(solution)/shard_map/all_to_all | solution.py:58
  516.3 15.4 %multiply_reduce_fusion.1 = (f32[]{:T(128)}, f32[64,64,256]{2,0,1:T(8,128)}) fusion(f32[64,64,256]{2,0,1:T(8,128)} %bitcast.125, f32[64]{0:T(128)S(1)} %get-tuple-element.16, f32[64]{0:T(128)S(1)} %get-tuple-element.17, f32[64,64,256]{2,1,0:T(8,128)} %param.4, f32[64,256]{1,0:T(8,128)S(1)} %get-tuple-element.11, f32[64,64,256]{2,1,0:T(8,128)} %param.5), kind=kOutput, calls=%fused_computation.23 | convolution fusion | flops 810569728 | bytes 16843268 | tf_op jit(solution)/shard_map/mj,jyx->myx/dot_general | solution.py:59
  540.9 19.3 %fusion.127 = f32[256,64,64]{2,1,0:T(8,128)} fusion(f32[64,64,256]{0,1,2:T(8,128)} %copy.89, f32[256,64,64]{2,1,0:T(8,128)} %copy.90), kind=kOutput, calls=%fused_computation.151 | convolution fusion | flops 805306368 | bytes 12582912 | tf_op jit(solution)/shard_map/xmn,nyx->myx/dot_general | solution.py:63
  588.0 17.7 %fusion.147 = f32[1024,1024,1]{1,0,2:T(8,128)} fusion(), kind=kLoop, calls=%fused_computation.13.clone | loop fusion | flops 16777216 | bytes 4194304 | tf_op jit(solution)/shard_map/zyk,xk->zyx/dot_general | solution.py:51
  605.7 30.5 %all-to-all-done.4 = f32[64,64,256]{2,1,0:T(8,128)} async-done(((f32[64,64,256]{2,1,0:T(8,128)}), f32[64,64,256]{2,1,0:T(8,128)}, u32[]{:S(2)}, u32[]{:S(2)}) %all-to-all-start.4) | async-done | bytes 4194336 | tf_op jit(solution)/shard_map/all_to_all | solution.py:50
  648.9 17.6 %fusion.7 = f32[16,64,1024]{2,1,0:T(8,128)} fusion(f32[16,64,1024]{2,1,0:T(8,128)} %all_to_all.123, f32[1024,1024,1]{1,0,2:T(8,128)} %fusion.147), kind=kOutput, calls=%fused_computation.12 | convolution fusion | flops 12884901888 | bytes 12582912 | tf_op jit(solution)/shard_map/zyk,xk->zyx/dot_general | solution.py:51
  684.5 97.7 %all_to_all.145 = f32[8,1,131072]{2,1,0:T(1,128)} all-to-all(f32[8,1,131072]{2,1,0:T(1,128)} %reshape.105), channel_id=1, replica_groups=mesh['px'=8,'py'=4] {'px'}, dimensions={0} | all-to-all | bytes 8388608 | tf_op jit(solution)/shard_map/all_to_all | solution.py:52
  811.5 19.9 %fusion.44 = f32[16,128,512]{2,1,0:T(8,128)S(1)} fusion(f32[16,512,128]{2,1,0:T(8,128)} %bitcast.127), kind=kOutput, calls=%fused_computation.57 | convolution fusion | flops 6446645248 | bytes 8388608 | tf_op jit(solution)/shard_map/zkx,yk->zxy/dot_general | solution.py:53
  831.5 16.5 %fusion.33 = f32[16,512,128]{2,1,0:T(8,128)S(1)} fusion(f32[16,128,512]{2,1,0:T(8,128)S(1)} %fusion.44, f32[16,128,512]{2,1,0:T(8,128)S(1)} %copy-done.2), kind=kOutput, calls=%fused_computation.45 | convolution fusion | flops 6450839552 | bytes 12582912 | tf_op jit(solution)/shard_map/zxy,ky->zkx/dot_general | solution.py:55
  857.3 17.7 %fusion.145 = f32[1024,1024,1]{1,0,2:T(8,128)} fusion(), kind=kLoop, calls=%fused_computation.11.clone.1 | loop fusion | flops 16777216 | bytes 4194304 | tf_op jit(solution)/shard_map/zyx,kx->zyk/dot_general | solution.py:57
  875.0 74.6 %all-to-all-done.6 = f32[16,512,128]{2,0,1:T(8,128)} async-done(((f32[16,512,128]{2,0,1:T(8,128)}), f32[16,512,128]{2,0,1:T(8,128)}, u32[]{:S(2)}, u32[]{:S(2)}) %all-to-all-start.6) | async-done | bytes 4194336 | tf_op jit(solution)/shard_map/all_to_all | solution.py:56
  961.0 17.6 %fusion.5 = f32[16,64,1024]{2,1,0:T(8,128)} fusion(f32[16,64,1024]{2,1,0:T(8,128)} %all_to_all.131, f32[1024,1024,1]{1,0,2:T(8,128)} %fusion.145), kind=kOutput, calls=%fused_computation.10 | convolution fusion | flops 12884901888 | bytes 12582912 | tf_op jit(solution)/shard_map/zyx,kx->zyk/dot_general | solution.py:57
  995.5 53.9 %all_to_all.146 = f32[4,1,262144]{2,1,0:T(1,128)} all-to-all(f32[4,1,262144]{2,1,0:T(1,128)} %reshape.107), channel_id=1, replica_groups=mesh['px'=8,'py'=4] {'py'}, dimensions={0} | all-to-all | bytes 8388608 | tf_op jit(solution)/shard_map/all_to_all | solution.py:58
  1104.8 19.4 %fusion.128 = f32[256,64,64]{2,1,0:T(8,128)} fusion(f32[64,64,256]{0,1,2:T(8,128)} %copy.104, f32[256,64,64]{2,1,0:T(8,128)} %copy.90), kind=kOutput, calls=%fused_computation.152 | convolution fusion | flops 805306368 | bytes 12582912 | tf_op jit(solution)/shard_map/xmn,nyx->myx/dot_general | solution.py:63
  1142.2 37.5 %psum.7 = f32[2]{0:T(128)S(1)} all-reduce(f32[2]{0:T(128)S(1)} %pad_maximum_fusion), channel_id=1, replica_groups=mesh['px'=8,'py'=4] {'px','py'}, use_global_device_ids=true, to_apply=%region_2.3 | all-reduce | flops 2 | bytes 16 | tf_op jit(solution)/shard_map/psum | solution.py:65
  (61 shorter events, 372.8 us)
Async XLA Ops:
  13.6 53.9 %all-to-all-start = ((f32[64,64,256]{2,1,0:T(8,128)}), f32[64,64,256]{2,1,0:T(8,128)}, u32[]{:S(2)}, u32[]{:S(2)}) async-start(f32[64,64,256]{2,1,0:T(8,128)} %copy.78), calls=%async_computation | async-start | bytes 8388608 | tf_op jit(solution)/shard_map/all_to_all | solution.py:50
  245.9 19.7 %copy-start.1 = (f32[16,128,512]{2,1,0:T(8,128)S(1)}, f32[16,128,512]{2,1,0:T(8,128)}, u32[]{:S(2)}) copy-start(f32[16,128,512]{2,1,0:T(8,128)} %param.6) | copy-start | bytes 12582916
  286.9 96.8 %all-to-all-start.2 = ((f32[16,512,128]{2,0,1:T(8,128)}), f32[16,512,128]{2,0,1:T(8,128)}, u32[]{:S(2)}, u32[]{:S(2)}) async-start(f32[16,512,128]{2,0,1:T(8,128)} %copy.84), calls=%async_computation.2 | async-start | bytes 8388608 | tf_op jit(solution)/shard_map/all_to_all | solution.py:56
  429.7 53.1 %all-to-all-start.3 = ((f32[4,1,262144]{2,1,0:T(1,128)}), f32[4,1,262144]{2,1,0:T(1,128)}, u32[]{:S(2)}, u32[]{:S(2)}) async-start(f32[4,1,262144]{2,1,0:T(1,128)} %reshape.103), calls=%async_computation.3 | async-start | bytes 8388608 | tf_op jit(solution)/shard_map/all_to_all | solution.py:58
  574.3 4.0 copy-start
  582.7 53.5 %all-to-all-start.4 = ((f32[64,64,256]{2,1,0:T(8,128)}), f32[64,64,256]{2,1,0:T(8,128)}, u32[]{:S(2)}, u32[]{:S(2)}) async-start(f32[64,64,256]{2,1,0:T(8,128)} %copy.93), calls=%async_computation.4 | async-start | bytes 8388608 | tf_op jit(solution)/shard_map/all_to_all | solution.py:50
  811.5 19.9 %copy-start.2 = (f32[16,128,512]{2,1,0:T(8,128)S(1)}, f32[16,128,512]{2,1,0:T(8,128)}, u32[]{:S(2)}) copy-start(f32[16,128,512]{2,1,0:T(8,128)} %param.6) | copy-start | bytes 12582916
  852.7 96.9 %all-to-all-start.6 = ((f32[16,512,128]{2,0,1:T(8,128)}), f32[16,512,128]{2,0,1:T(8,128)}, u32[]{:S(2)}, u32[]{:S(2)}) async-start(f32[16,512,128]{2,0,1:T(8,128)} %copy.99), calls=%async_computation.6 | async-start | bytes 8388608 | tf_op jit(solution)/shard_map/all_to_all | solution.py:56
where the time goes:
time: 1190 us; the launch traced here: 1180 us
  blocking collectives  289 us (24%)
  local copies, waits for them, and re-layouts  252 us (21%)
  waiting for transfers between devices  250 us (21%)
  matrix products  223 us (19%)
  other arithmetic  141 us (12%)
  starting transfers between devices  24.4 us (2%)
    all_to_all x2, blocking collectives, local(): lax.all_to_all(lines, 'px', split_axis=2, concat_axis=1, tiled=True)  197 us
    all_to_all x2, waiting for transfers between devices, local(): lax.all_to_all(returned, 'px', split_axis=1, concat_axis=2, tiled=True)  149 us
    unnamed x16, local copies, waits for them, and re-layouts  86.7 us
    all_to_all x2, waiting for transfers between devices, local(): lax.all_to_all(points, 'py', split_axis=0, concat_axis=2, tiled=True)  61.6 us
    all_to_all x1, blocking collectives, local(): lax.all_to_all(returned, 'py', split_axis=2, concat_axis=0, tiled=True)  53.9 us
    dot_general x2, matrix products, local(): physical = jnp.einsum('zkx,yk->zxy', columns, table_y, precision=highest)  39.6 us
    all_to_all x1, waiting for transfers between devices, local(): lax.all_to_all(returned, 'py', split_axis=2, concat_axis=0, tiled=True)  38.9 us
    dot_general x2, matrix products, local(): jnp.einsum('xmn,nyx->myx', depth_inverse, residual, precision=highest)  38.7 us
  transfers between devices with their start and end apart: 5, of which 5 were waited for; matrix products, arithmetic and copies ran while one was open for 7% of the time, Pallas kernels for 0%

commit v1 on v0

--- a/solution.py
+++ b/solution.py
@@ -55,7 +55,10 @@
         returned = jnp.einsum("zxy,ky->zkx", stress, table_y, precision=highest)
         returned = lax.all_to_all(returned, "px", split_axis=1, concat_axis=2, tiled=True)
         returned = jnp.einsum("zyx,kx->zyk", returned, table_x, precision=highest)
-        spectral = lax.all_to_all(returned, "py", split_axis=2, concat_axis=0, tiled=True)
+        spectral = jnp.concatenate(
+            lax.all_to_all(jnp.stack(jnp.split(returned, lax.axis_size("py"), axis=2)), "py", 0, 0),
+            axis=0,
+        )
         viscous = jnp.einsum("mj,jyx->myx", backward, spectral, precision=highest)
         residual = forcing - (lateral * field + viscous)
         squares = jnp.sum(residual * residual)

time: 1190 us -> 1090 us (0.916)
  local copies, waits for them, and re-layouts: 252 us -> 184 us
  other arithmetic: 141 us -> 114 us
    unnamed x16, local copies, waits for them, and re-layouts: 86.7 us -> 50.6 us
    all_to_all x2 -> x0, other arithmetic: 30.5 us -> none  [local(): lax.all_to_all(returned, 'py', split_axis=2, concat_axis=0, tiled=True)]
    all_to_all x2 -> x0, local copies, waits for them, and re-layouts: 17.4 us -> none  [local(): lax.all_to_all(returned, 'py', split_axis=2, concat_axis=0, tiled=True)]
    dot_general x2 -> x0, local copies, waits for them, and re-layouts: 16.2 us -> none  [local(): returned = jnp.einsum('zyx,kx->zyk', returned, table_x, precision=highest)]
where the time goes in v1:
time: 1090 us; the launch traced here: 1080 us
  blocking collectives  286 us (26%)
  waiting for transfers between devices  250 us (23%)
  matrix products  220 us (20%)
  local copies, waits for them, and re-layouts  184 us (17%)
  other arithmetic  114 us (10%)
  starting transfers between devices  24.4 us (2%)
    all_to_all x2, blocking collectives, local(): lax.all_to_all(lines, 'px', split_axis=2, concat_axis=1, tiled=True)  197 us
    all_to_all x2, waiting for transfers between devices, local(): lax.all_to_all(returned, 'px', split_axis=1, concat_axis=2, tiled=True)  149 us
    all_to_all x2, waiting for transfers between devices, local(): lax.all_to_all(points, 'py', split_axis=0, concat_axis=2, tiled=True)  61.7 us
    all_to_all x1, blocking collectives, local(): lax.all_to_all(jnp.stack(jnp.split(returned, lax.axis_size('py'), axis=2)...  51.3 us
    unnamed x16, local copies, waits for them, and re-layouts  50.6 us
    dot_general x2, matrix products, local(): physical = jnp.einsum('zkx,yk->zxy', columns, table_y, precision=highest)  39.5 us
    all_to_all x1, waiting for transfers between devices, local(): lax.all_to_all(jnp.stack(jnp.split(returned, lax.axis_size('py'), axis=2)...  38.9 us
    dot_general x2, matrix products, local(): jnp.einsum('xmn,nyx->myx', depth_inverse, residual, precision=highest)  38.3 us
  transfers between devices with their start and end apart: 5, of which 5 were waited for; matrix products, arithmetic and copies ran while one was open for 7% of the time, Pallas kernels for 0%

profile of v1, /device:TPU:0, one launch (start us, length us, event | category | flops | bytes accessed | tf_op | source)
XLA Modules:
  0.0 1079.8 jit_solution(10654087167274354473)
XLA Ops:
  18.7 17.7 %fusion.157 = f32[1024,1024,1]{1,0,2:T(8,128)} fusion(), kind=kLoop, calls=%fused_computation.19.clone | loop fusion | flops 16777216 | bytes 4194304 | tf_op jit(solution)/shard_map/zyk,xk->zyx/dot_general | solution.py:51
  36.3 31.2 %all-to-all-done = f32[64,64,256]{2,1,0:T(8,128)} async-done(((f32[64,64,256]{2,1,0:T(8,128)}), f32[64,64,256]{2,1,0:T(8,128)}, u32[]{:S(2)}, u32[]{:S(2)}) %all-to-all-start) | async-done | bytes 4194336 | tf_op jit(solution)/shard_map/all_to_all | solution.py:50
  80.4 17.6 %fusion.11 = f32[16,64,1024]{2,1,0:T(8,128)} fusion(f32[16,64,1024]{2,1,0:T(8,128)} %all_to_all.87, f32[1024,1024,1]{1,0,2:T(8,128)} %fusion.157), kind=kOutput, calls=%fused_computation.18 | convolution fusion | flops 12884901888 | bytes 12582912 | tf_op jit(solution)/shard_map/zyk,xk->zyx/dot_general | solution.py:51
  116.2 99.8 %all_to_all.118 = f32[8,1,131072]{2,1,0:T(1,128)} all-to-all(f32[8,1,131072]{2,1,0:T(1,128)} %reshape.109), channel_id=1, replica_groups=mesh['px'=8,'py'=4] {'px'}, dimensions={0} | all-to-all | bytes 8388608 | tf_op jit(solution)/shard_map/all_to_all | solution.py:52
  245.9 19.7 %fusion.55 = f32[16,128,512]{2,1,0:T(8,128)S(1)} fusion(f32[16,512,128]{2,1,0:T(8,128)} %bitcast.125), kind=kOutput, calls=%fused_computation.74 | convolution fusion | flops 6446645248 | bytes 8388608 | tf_op jit(solution)/shard_map/zkx,yk->zxy/dot_general | solution.py:53
  265.7 16.8 %fusion.34 = f32[16,512,128]{2,1,0:T(8,128)S(1)} fusion(f32[16,128,512]{2,1,0:T(8,128)S(1)} %fusion.55, f32[16,128,512]{2,1,0:T(8,128)S(1)} %copy-done.2), kind=kOutput, calls=%fused_computation.50 | convolution fusion | flops 6450839552 | bytes 12582912 | tf_op jit(solution)/shard_map/zxy,ky->zkx/dot_general | solution.py:55
  291.7 17.7 %fusion.155 = f32[1024,1024,1]{1,0,2:T(8,128)} fusion(), kind=kLoop, calls=%fused_computation.17.clone | loop fusion | flops 16777216 | bytes 4194304 | tf_op jit(solution)/shard_map/zyx,kx->zyk/dot_general | solution.py:57
  309.3 74.6 %all-to-all-done.2 = f32[16,512,128]{2,0,1:T(8,128)} async-done(((f32[16,512,128]{2,0,1:T(8,128)}), f32[16,512,128]{2,0,1:T(8,128)}, u32[]{:S(2)}, u32[]{:S(2)}) %all-to-all-start.2) | async-done | bytes 4194336 | tf_op jit(solution)/shard_map/all_to_all | solution.py:56
  395.5 16.9 %fusion.9 = f32[16,64,1024]{2,1,0:T(8,128)S(1)} fusion(f32[16,64,1024]{2,1,0:T(8,128)} %all_to_all.95, f32[1024,1024,1]{1,0,2:T(8,128)} %fusion.155), kind=kOutput, calls=%fused_computation.16 | convolution fusion | flops 12884901888 | bytes 12582912 | tf_op jit(solution)/shard_map/zyx,kx->zyk/dot_general | solution.py:57
  429.9 38.9 %all-to-all-done.3 = f32[4,16,64,256]{3,2,1,0:T(8,128)} async-done(((f32[4,16,64,256]{3,2,1,0:T(8,128)}), f32[4,16,64,256]{3,2,1,0:T(8,128)}, u32[]{:S(2)}, u32[]{:S(2)}) %all-to-all-start.3) | async-done | bytes 4194336 | tf_op jit(solution)/shard_map/all_to_all | solution.py:59
  468.8 17.3 %multiply_reduce_fusion.1 = (f32[]{:T(128)}, f32[64,64,256]{2,0,1:T(8,128)}) fusion(f32[64,64,256]{2,1,0:T(8,128)} %bitcast.17, f32[64]{0:T(128)S(1)} %or_select_fusion, f32[64]{0:T(128)S(1)} %iota_multiply_fusion, f32[64,64,256]{2,1,0:T(8,128)} %param.4, f32[64,256]{1,0:T(8,128)S(1)} %get-tuple-element.19, f32[64,64,256]{2,1,0:T(8,128)} %param.5), kind=kOutput, calls=%fused_computation.29 | convolution fusion | flops 810569728 | bytes 16843268 | tf_op jit(solution)/shard_map/mj,jyx->myx/dot_general | solution.py:62
  495.6 19.2 %fusion.135 = f32[256,64,64]{2,1,0:T(8,128)} fusion(f32[64,64,256]{0,1,2:T(8,128)} %copy.86, f32[256,64,64]{2,1,0:T(8,128)} %copy.87), kind=kOutput, calls=%fused_computation.165 | convolution fusion | flops 805306368 | bytes 12582912 | tf_op jit(solution)/shard_map/xmn,nyx->myx/dot_general | solution.py:66
  542.3 17.7 %fusion.153 = f32[1024,1024,1]{1,0,2:T(8,128)} fusion(), kind=kLoop, calls=%fused_computation.15.clone | loop fusion | flops 16777216 | bytes 4194304 | tf_op jit(solution)/shard_map/zyk,xk->zyx/dot_general | solution.py:51
  560.0 30.5 %all-to-all-done.4 = f32[64,64,256]{2,1,0:T(8,128)} async-done(((f32[64,64,256]{2,1,0:T(8,128)}), f32[64,64,256]{2,1,0:T(8,128)}, u32[]{:S(2)}, u32[]{:S(2)}) %all-to-all-start.4) | async-done | bytes 4194336 | tf_op jit(solution)/shard_map/all_to_all | solution.py:50
  603.2 17.6 %fusion.7 = f32[16,64,1024]{2,1,0:T(8,128)} fusion(f32[16,64,1024]{2,1,0:T(8,128)} %all_to_all.100, f32[1024,1024,1]{1,0,2:T(8,128)} %fusion.153), kind=kOutput, calls=%fused_computation.14 | convolution fusion | flops 12884901888 | bytes 12582912 | tf_op jit(solution)/shard_map/zyk,xk->zyx/dot_general | solution.py:51
  639.0 97.7 %all_to_all.119 = f32[8,1,131072]{2,1,0:T(1,128)} all-to-all(f32[8,1,131072]{2,1,0:T(1,128)} %reshape.111), channel_id=1, replica_groups=mesh['px'=8,'py'=4] {'px'}, dimensions={0} | all-to-all | bytes 8388608 | tf_op jit(solution)/shard_map/all_to_all | solution.py:52
  766.0 19.7 %fusion.52 = f32[16,128,512]{2,1,0:T(8,128)S(1)} fusion(f32[16,512,128]{2,1,0:T(8,128)} %bitcast.126), kind=kOutput, calls=%fused_computation.71 | convolution fusion | flops 6446645248 | bytes 8388608 | tf_op jit(solution)/shard_map/zkx,yk->zxy/dot_general | solution.py:53
  785.7 16.8 %fusion.37 = f32[16,512,128]{2,1,0:T(8,128)S(1)} fusion(f32[16,128,512]{2,1,0:T(8,128)S(1)} %fusion.52, f32[16,128,512]{2,1,0:T(8,128)S(1)} %copy-done.3), kind=kOutput, calls=%fused_computation.51 | convolution fusion | flops 6450839552 | bytes 12582912 | tf_op jit(solution)/shard_map/zxy,ky->zkx/dot_general | solution.py:55
  811.6 17.7 %fusion.151 = f32[1024,1024,1]{1,0,2:T(8,128)} fusion(), kind=kLoop, calls=%fused_computation.13.clone.1 | loop fusion | flops 16777216 | bytes 4194304 | tf_op jit(solution)/shard_map/zyx,kx->zyk/dot_general | solution.py:57
  829.3 74.6 %all-to-all-done.6 = f32[16,512,128]{2,0,1:T(8,128)} async-done(((f32[16,512,128]{2,0,1:T(8,128)}), f32[16,512,128]{2,0,1:T(8,128)}, u32[]{:S(2)}, u32[]{:S(2)}) %all-to-all-start.6) | async-done | bytes 4194336 | tf_op jit(solution)/shard_map/all_to_all | solution.py:56
  915.4 16.9 %fusion.5 = f32[16,64,1024]{2,1,0:T(8,128)S(1)} fusion(f32[16,64,1024]{2,1,0:T(8,128)} %all_to_all.108, f32[1024,1024,1]{1,0,2:T(8,128)} %fusion.151), kind=kOutput, calls=%fused_computation.12 | convolution fusion | flops 12884901888 | bytes 12582912 | tf_op jit(solution)/shard_map/zyx,kx->zyk/dot_general | solution.py:57
  933.2 51.3 %all_to_all.120 = f32[4,16,64,256]{3,2,1,0:T(8,128)S(1)} all-to-all(f32[4,16,64,256]{3,2,1,0:T(8,128)S(1)} %pad_maximum_fusion.1), channel_id=1, replica_groups=mesh['px'=8,'py'=4] {'py'}, dimensions={0} | all-to-all | bytes 8388608 | tf_op jit(solution)/shard_map/all_to_all | solution.py:59
  996.0 37.5 %psum.7 = f32[2]{0:T(128)S(1)} all-reduce(f32[2]{0:T(128)S(1)} %pad_maximum_fusion.2), channel_id=1, replica_groups=mesh['px'=8,'py'=4] {'px','py'}, use_global_device_ids=true, to_apply=%region_2.3 | all-reduce | flops 2 | bytes 16 | tf_op jit(solution)/shard_map/psum | solution.py:68
  1043.2 19.2 %fusion.136 = f32[256,64,64]{2,1,0:T(8,128)} fusion(f32[64,64,256]{0,1,2:T(8,128)} %copy.100, f32[256,64,64]{2,1,0:T(8,128)} %copy.87), kind=kOutput, calls=%fused_computation.166 | convolution fusion | flops 805306368 | bytes 12582912 | tf_op jit(solution)/shard_map/xmn,nyx->myx/dot_general | solution.py:66
  (60 shorter events, 273.9 us)
Async XLA Ops:
  13.6 54.0 %all-to-all-start = ((f32[64,64,256]{2,1,0:T(8,128)}), f32[64,64,256]{2,1,0:T(8,128)}, u32[]{:S(2)}, u32[]{:S(2)}) async-start(f32[64,64,256]{2,1,0:T(8,128)} %copy.76), calls=%async_computation | async-start | bytes 8388608 | tf_op jit(solution)/shard_map/all_to_all | solution.py:50
  245.9 19.8 %copy-start.2 = (f32[16,128,512]{2,1,0:T(8,128)S(1)}, f32[16,128,512]{2,1,0:T(8,128)}, u32[]{:S(2)}) copy-start(f32[16,128,512]{2,1,0:T(8,128)} %param.6) | copy-start | bytes 12582916
  287.1 96.8 %all-to-all-start.2 = ((f32[16,512,128]{2,0,1:T(8,128)}), f32[16,512,128]{2,0,1:T(8,128)}, u32[]{:S(2)}, u32[]{:S(2)}) async-start(f32[16,512,128]{2,0,1:T(8,128)} %copy.82), calls=%async_computation.2 | async-start | bytes 8388608 | tf_op jit(solution)/shard_map/all_to_all | solution.py:56
  415.5 53.3 %all-to-all-start.3 = ((f32[4,16,64,256]{3,2,1,0:T(8,128)}), f32[4,16,64,256]{3,2,1,0:T(8,128)}, u32[]{:S(2)}, u32[]{:S(2)}) async-start(f32[4,16,64,256]{3,2,1,0:T(8,128)} %pad_maximum_fusion), calls=%async_computation.3 | async-start | bytes 8388608 | tf_op jit(solution)/shard_map/all_to_all | solution.py:59
  528.8 4.0 copy-start
  537.2 53.3 %all-to-all-start.4 = ((f32[64,64,256]{2,1,0:T(8,128)}), f32[64,64,256]{2,1,0:T(8,128)}, u32[]{:S(2)}, u32[]{:S(2)}) async-start(f32[64,64,256]{2,1,0:T(8,128)} %copy.90), calls=%async_computation.4 | async-start | bytes 8388608 | tf_op jit(solution)/shard_map/all_to_all | solution.py:50
  766.0 19.8 %copy-start.3 = (f32[16,128,512]{2,1,0:T(8,128)S(1)}, f32[16,128,512]{2,1,0:T(8,128)}, u32[]{:S(2)}) copy-start(f32[16,128,512]{2,1,0:T(8,128)} %param.6) | copy-start | bytes 12582916
  807.1 96.9 %all-to-all-start.6 = ((f32[16,512,128]{2,0,1:T(8,128)}), f32[16,512,128]{2,0,1:T(8,128)}, u32[]{:S(2)}, u32[]{:S(2)}) async-start(f32[16,512,128]{2,0,1:T(8,128)} %copy.96), calls=%async_computation.6 | async-start | bytes 8388608 | tf_op jit(solution)/shard_map/all_to_all | solution.py:56
  933.2 51.3 %copy-start.1 = (f32[64,64,256]{2,0,1:T(8,128)S(1)}, f32[64,64,256]{2,0,1:T(8,128)}, u32[]{:S(2)}) copy-start(f32[64,64,256]{2,0,1:T(8,128)} %copy-done) | copy-start | bytes 12582916
  933.2 51.3 %copy-start.4 = (f32[64,64,256]{2,1,0:T(8,128)S(1)}, f32[64,64,256]{2,1,0:T(8,128)}, u32[]{:S(2)}) copy-start(f32[64,64,256]{2,1,0:T(8,128)} %param.5) | copy-start | bytes 12582916
